TPU v7x, 512 devices: a whole 4x4x16 slice. The times are simulated.
512 devices in a mesh: grp: 16 (over y, z_hi, core), dev: 32 (over z_lo, x).
Axes of the slice: x: 4, y: 4, z: 16 (z_hi: 2, z_lo: 8; z = z_hi * 8 + z_lo), core: 2. Of those that a mesh axis runs over, the one named last changes fastest.
Arguments:
- train_grads: bfloat16 [65536, 1024], P(('grp', 'dev')), may hold values from -192 to 192, as said below
- queries: bfloat16 [2048, 1024], P('grp'), may hold values from -6 to 6
Outputs:
- scores: bfloat16 [65536, 2048], P(('grp', 'dev'))
Inputs may be any that keep to these rules, and one draw needn't show every extreme that they name: `train_grads`: Real-valued projected gradients whose columns and rows differ in scale.
All inputs are finite; a program needn't handle non-finite values. Where the computation divides by a largest or mean magnitude, that divisor is 1e-20 or more.
Results may differ from a plain program's by a relative error of at most 0.001.
The roundings to bfloat16 on the way count: a program that leaves them out, or rounds other values in their place, can miss the bound.
Values may be sent and summed in bfloat16 or wider, within the bound.
A program may use at most 64 MiB of HBM per device.

v0:
```python
import jax
import jax.numpy as jnp
from jax import lax
from jax.sharding import PartitionSpec as P

ITERS = 8
damping_ratio = 0.1


def copy_for_each(array, axis):
    copies = jnp.broadcast_to(array, (lax.axis_size(axis), *array.shape))
    return lax.all_to_all(copies, axis, split_axis=0, concat_axis=0, tiled=True)


def laid_out(pieces, dim):
    dims = list(pieces.shape[1:])
    dims[dim] *= pieces.shape[0]
    return jnp.moveaxis(pieces, 0, dim).reshape(dims)


def gather_directly(array, axis, dim):
    pieces = copy_for_each(array, axis)
    return laid_out(pieces, dim)


def local_solve(gram, own, total, width):
    normed = gram / total
    damp = damping_ratio * jnp.trace(gram) / (total * width)
    bound = jnp.max(jnp.sum(jnp.abs(normed), axis=1)) + damp
    step = 1.0 / bound
    oper = normed + damp * jnp.eye(width, dtype=jnp.float32)
    state = step * own
    for index in range(ITERS):
        state = state + step * (own - jnp.dot(state, oper, precision=lax.Precision.HIGHEST))
    return state.astype(jnp.bfloat16)


def body(train_grads, queries):
    rows, width = train_grads.shape
    ndevice = lax.axis_size("dev")
    total = rows * ndevice * lax.axis_size("grp")
    qvals = queries.astype(jnp.float32)
    qrows = qvals.shape[0] // ndevice
    qstart = lax.axis_index("dev") * qrows
    own = lax.dynamic_slice_in_dim(qvals, qstart, qrows, 0)
    gram = lax.psum(
        lax.dot_general(
            train_grads, train_grads, (((0,), (0,)), ((), ())), preferred_element_type=jnp.float32
        ),
        ("grp", "dev"),
    )
    mine = local_solve(gram, own, total, width)
    prepared = gather_directly(mine, "dev", 0)
    return lax.dot_general(
        train_grads,
        lax.all_gather(prepared, "grp", axis=0, tiled=True),
        (((1,), (1,)), ((), ())),
        preferred_element_type=jnp.float32,
    ).astype(jnp.bfloat16)


def solution(mesh):
    return jax.shard_map(
        body,
        mesh=mesh,
        in_specs=(P(("grp", "dev"), None), P("grp", None)),
        out_specs=P(("grp", "dev"), None),
        check_vma=False,
    )
```

profile of v0, /device:TPU:1, one launch (start us, length us, event | category | flops | bytes accessed | tf_op | source)
XLA Modules:
  0.0 696.8 jit_solution(398364279938283323)
XLA Ops:
  6.5 0.0 copy-start
  6.5 0.0 all-reduce.2.cloned.1.call-start
  6.5 0.9 copy-done
  7.5 2.7 fusion.19
  10.2 0.0 all-reduce.2.cloned.1.call-update
  10.2 0.0 all-gather.2.cloned.1.call-start
  10.3 500.9 %all-reduce.2.cloned.1.call-done = f32[1024,1024]{1,0:T(8,128)} async-done(((f32[1024,1024]{1,0:T(8,128)}), f32[1024,1024]{1,0:T(8,128)}) %all-reduce.2.cloned.1.call-update) | async-done | bytes 4194320 | tf_op jit(solution)/shard_map/psum | solution.py:46
  511.2 3.3 select_reduce_fusion
  515.2 0.6 reduce_max.9
  516.5 0.0 copy-start.1
  516.5 4.6 fusion.16
  521.1 0.0 copy-done.1
  521.1 3.0 fusion.14
  524.1 3.0 fusion.12
  527.0 3.0 fusion.10
  530.0 3.0 fusion.8
  532.9 3.1 fusion.6
  536.1 3.0 fusion.4
  539.0 3.0 fusion.17
  542.0 0.1 broadcast_in_dim.8
  542.1 31.9 %all_to_all.5 = bf16[32,4,1024]{2,1,0:T(4,128)(2,1)S(1)} all-to-all(bf16[32,4,1024]{2,1,0:T(4,128)(2,1)S(1)} %broadcast_in_dim.8), channel_id=1, replica_groups=mesh['grp'=16,'dev'=32] {'dev'}, dimensions={0} | all-to-all | bytes 524288 | tf_op jit(solution)/shard_map/all_to_all | solution.py:12
  574.0 0.8 reshape.3
  574.8 0.0 all-gather.2.cloned.1.call-update
  574.8 110.7 %all-gather.2.cloned.1.call-done = bf16[2048,1024]{1,0:T(8,128)(2,1)} async-done(((bf16[128,1024]{1,0:T(8,128)(2,1)}), bf16[2048,1024]{1,0:T(8,128)(2,1)}) %all-gather.2.cloned.1.call-update) | async-done | bytes 4194320 | tf_op jit(solution)/shard_map/all_gather | solution.py:56
  685.5 3.4 fusion
  689.0 1.0 copy.3
Async XLA Ops:
  6.5 1.0 copy-start
  6.5 504.7 %all-reduce.2.cloned.1.call-start = ((), (), s32[]{:S(2)}) async-start(), calls=%async_computation.1 | async-start | bytes 8388608 | tf_op jit(solution)/shard_map/psum | solution.py:46
  10.2 675.3 %all-gather.2.cloned.1.call-start = ((), (), s32[]{:S(2)}) async-start(), calls=%async_computation.2 | async-start | bytes 4456448 | tf_op jit(solution)/shard_map/all_gather | solution.py:56
  516.5 4.6 copy-start.1
Sparse Core Ops, SparseCore 0:
  12.8 498.3 all-reduce.1
  574.9 110.5 all-gather.1
where the time goes:
time: 698 us; the launch traced here: 697 us
  waiting for transfers between devices  612 us (88%)
  blocking collectives  31.9 us (5%)
  matrix products  31.6 us (5%)
  between operations  14.8 us (2%)
    psum x1, waiting for transfers between devices, body(): lax.psum(lax.dot_general(train_grads, train_grads, (((0,), (0,)), ((), ()...  501 us
    all_gather x1, waiting for transfers between devices, body(): lax.all_gather(prepared, 'grp', axis=0, tiled=True)  111 us
    all_to_all x1, blocking collectives, copy_for_each(): return lax.all_to_all(copies, axis, split_axis=0, concat_axis=0, tiled=True)  31.9 us
    dot_general x8, matrix products, local_solve(): jnp.dot(state, oper, precision=lax.Precision.HIGHEST)  25.5 us
  transfers between devices with their start and end apart: 2, of which 2 were waited for; matrix products, arithmetic and copies ran while one was open for 0% of the time, Pallas kernels for 0%

commit v1 on v0

--- a/solution.py
+++ b/solution.py
@@ -53,7 +53,9 @@
     prepared = gather_directly(mine, "dev", 0)
     return lax.dot_general(
         train_grads,
-        lax.all_gather(prepared, "grp", axis=0, tiled=True),
+        jnp.concatenate(
+            lax.all_to_all(jnp.stack([prepared] * lax.axis_size("grp")), "grp", 0, 0), axis=0
+        ),
         (((1,), (1,)), ((), ())),
         preferred_element_type=jnp.float32,
     ).astype(jnp.bfloat16)

time: 698 us -> 782 us (1.12)
  the two profiles are of different devices: /device:TPU:1 before, /device:TPU:32 now
where the time goes in v1:
time: 782 us; the launch traced here: 781 us
  waiting for transfers between devices  499 us (64%)
  blocking collectives  231 us (30%)
  matrix products  29.4 us (4%)
  between operations  14.8 us (2%)
    psum x1, waiting for transfers between devices, body(): lax.psum(lax.dot_general(train_grads, train_grads, (((0,), (0,)), ((), ()...  499 us
    all_to_all x1, blocking collectives, body(): lax.all_to_all(jnp.stack([prepared] * lax.axis_size('grp')), 'grp', 0, 0)  203 us
    all_to_all x1, blocking collectives, copy_for_each(): return lax.all_to_all(copies, axis, split_axis=0, concat_axis=0, tiled=True)  28.3 us
    dot_general x8, matrix products, local_solve(): jnp.dot(state, oper, precision=lax.Precision.HIGHEST)  25.5 us
  transfers between devices with their start and end apart: 1, of which 1 were waited for; matrix products, arithmetic and copies ran while one was open for 0% of the time, Pallas kernels for 0%

profile of v1, /device:TPU:32, one launch (start us, length us, event | category | flops | bytes accessed | tf_op | source)
XLA Modules:
  0.0 781.3 jit_solution(8021927225910108518)
XLA Ops:
  6.5 0.0 copy-start
  6.5 0.0 all-reduce.2.cloned.1.call-start
  6.5 0.9 copy-done
  7.5 2.7 fusion.19
  10.2 0.0 all-reduce.2.cloned.1.call-update
  10.2 499.5 %all-reduce.2.cloned.1.call-done = f32[1024,1024]{1,0:T(8,128)} async-done(((f32[1024,1024]{1,0:T(8,128)}), f32[1024,1024]{1,0:T(8,128)}) %all-reduce.2.cloned.1.call-update) | async-done | bytes 4194320 | tf_op jit(solution)/shard_map/psum | solution.py:46
  509.7 3.3 select_reduce_fusion
  513.7 0.6 reduce_max.9
  514.9 0.0 copy-start.1
  515.0 4.6 fusion.16
  519.5 0.0 copy-done.1
  519.6 3.0 fusion.14
  522.5 3.0 fusion.12
  525.5 3.0 fusion.10
  528.4 3.0 fusion.8
  531.4 3.1 fusion.6
  534.5 3.0 fusion.4
  537.5 3.0 fusion.17
  540.5 0.1 broadcast_in_dim.8
  540.6 28.3 %all_to_all.10 = bf16[32,4,1024]{2,1,0:T(4,128)(2,1)S(1)} all-to-all(bf16[32,4,1024]{2,1,0:T(4,128)(2,1)S(1)} %broadcast_in_dim.8), channel_id=1, replica_groups=mesh['grp'=16,'dev'=32] {'dev'}, dimensions={0} | all-to-all | bytes 524288 | tf_op jit(solution)/shard_map/all_to_all | solution.py:12
  568.9 0.1 stack_reshape.2
  568.9 0.5 stack.3
  569.5 202.7 %all_to_all.11 = bf16[16,128,1024]{2,1,0:T(8,128)(2,1)S(1)} all-to-all(bf16[16,128,1024]{2,1,0:T(8,128)(2,1)S(1)} %stack.3), channel_id=1, replica_groups=mesh['grp'=16,'dev'=32] {'grp'}, dimensions={0} | all-to-all | bytes 8388608 | tf_op jit(solution)/shard_map/all_to_all | solution.py:57
  772.2 1.3 fusion
  773.4 1.0 copy.3
Async XLA Ops:
  6.5 1.0 copy-start
  6.5 503.1 %all-reduce.2.cloned.1.call-start = ((), (), s32[]{:S(2)}) async-start(), calls=%async_computation.2 | async-start | bytes 8388608 | tf_op jit(solution)/shard_map/psum | solution.py:46
  514.9 4.6 copy-start.1
Sparse Core Ops, SparseCore 0:
  12.8 496.8 all-reduce.1
